TPU v7x, 32 devices: a whole 2x2x4 slice. The times are simulated.
32 devices in a mesh: member: 2 (over y), lat: 4 (over z), lon: 2 (over x), lev: 2 (over core).
Axes of the slice: x: 2, y: 2, z: 4, core: 2. Of those that a mesh axis runs over, the one named last changes fastest.
Arguments:
- perturbation: bfloat16 [4, 64, 16, 8, 128], P('member', 'lev', 'lat', 'lon'), parts along dimension 0, may hold values from -6 to 6
- adjoint_forcing: bfloat16 [4, 64, 16, 8, 128], P('member', 'lev', 'lat', 'lon'), parts along dimension 0, may hold values from -6 to 6
- source_rows: int32 [16, 8, 4], P('lat', 'lon'), may hold values from 0 to 15, as said below
- source_cols: int32 [16, 8, 4], P('lat', 'lon'), may hold values from 0 to 7, as said below
- cubic_weights: bfloat16 [16, 8, 4, 128, 128], P('lat', 'lon'), may hold values from -1.5 to 1.5
Outputs:
- tangent_out: bfloat16 [4, 64, 16, 8, 128], P('member', 'lev', 'lat', 'lon'), parts along dimension 0
- adjoint_out: bfloat16 [4, 64, 16, 8, 128], P('member', 'lev', 'lat', 'lon'), parts along dimension 0
There are 2 independent parts, one for each index of `member`. A program takes and returns all parts, laid end to end along the dimension named above; an argument that names none is the same for every part. Nothing has to cross between parts.
Inputs may be any that keep to these rules, and one draw needn't show every extreme that they name: source_rows[i, j, k] differs from i by at most 8. source_cols[i, j, k] is j + d modulo 8 with d from -1 to 1, and from -2 to 2 where i lies in the first or last 4 block rows.
All inputs are finite; a program needn't handle non-finite values.
Results may differ from a plain program's by a relative error of at most 0.004.
Values may be sent and summed in bfloat16 or wider, within the bound.
A program may use at most 64 MiB of HBM per device.

v0:
```python
import jax
import jax.numpy as jnp
from jax import lax
from jax.sharding import PartitionSpec as P


def passed_along(array, axis, by):
    devices = lax.axis_size(axis)
    pairs = [(i, i + by) for i in range(devices) if 0 <= i + by < devices]
    return lax.ppermute(array, axis, pairs)


def padded(cells, sides, width):
    for axis, dim in sides:
        count = lax.axis_size(axis)
        head = lax.slice_in_dim(cells, 0, width, axis=dim)
        tail = lax.slice_in_dim(cells, cells.shape[dim] - width, cells.shape[dim], axis=dim)
        cells = jnp.concatenate(
            [
                lax.ppermute(tail, axis, [(i, (i + 1) % count) for i in range(count)]),
                cells,
                lax.ppermute(head, axis, [((i + 1) % count, i) for i in range(count)]),
            ],
            axis=dim,
        )
    return cells


def shifted(array, axis, by):
    devices = lax.axis_size(axis)
    return lax.ppermute(array, axis, [(i, (i + by) % devices) for i in range(devices)])


def rows_extend(tile_data):
    return jnp.concatenate(
        [
            passed_along(tile_data, "lat", 2),
            passed_along(tile_data, "lat", 1),
            tile_data,
            passed_along(tile_data, "lat", -1),
            passed_along(tile_data, "lat", -2),
        ],
        axis=2,
    )


def cols_extend(tile_data):
    return padded(tile_data, (("lon", 3),), 2)


def on_device(perturbation, adjoint_forcing, source_rows, source_cols, cubic_weights):
    fields, levels, band_rows, tile_cols, cell_count = perturbation.shape
    stencil = source_rows.shape[2]
    reach_rows = 2 * band_rows
    row_count = fields * levels
    span_cols = tile_cols + 4
    height = band_rows + 2 * reach_rows
    places = height * span_cols
    targets = band_rows * tile_cols
    extended = cols_extend(rows_extend(perturbation))
    flattened = extended.reshape(row_count, places, cell_count)
    band_index = lax.axis_index("lat")
    tile_index = lax.axis_index("lon")
    total_cols = tile_cols * lax.axis_size("lon")
    local_rows = source_rows - band_index * band_rows + reach_rows
    local_cols = jnp.mod(source_cols - tile_index * tile_cols + 2, total_cols)
    positions = (local_rows * span_cols + local_cols).reshape(-1)
    gathered = jnp.take(flattened, positions, axis=1).reshape(
        row_count, targets, stencil, cell_count
    )
    weights = cubic_weights.reshape(targets, stencil, cell_count, cell_count)
    tangent = jnp.einsum("rtks,tksc->rtc", gathered, weights, preferred_element_type=jnp.float32)
    tangent_out = tangent.astype(jnp.bfloat16).reshape(
        fields, levels, band_rows, tile_cols, cell_count
    )
    forcing = adjoint_forcing.reshape(row_count, targets, cell_count)
    contributions = jnp.einsum(
        "rtc,tksc->rtks", forcing, weights, preferred_element_type=jnp.float32
    )
    contributions = contributions.reshape(row_count, targets * stencil, cell_count)
    onehot = (positions[:, None] == jnp.arange(places, dtype=jnp.int32)[None, :]).astype(
        jnp.float32
    )
    spread = jnp.einsum("rms,mn->rns", contributions, onehot, precision=lax.Precision.HIGHEST)
    spread = spread.reshape(row_count, height, span_cols, cell_count)
    from_east = shifted(spread[:, :, 0:2].astype(jnp.bfloat16), "lon", -1).astype(jnp.float32)
    from_west = shifted(spread[:, :, span_cols - 2 : span_cols], "lon", 1)
    inner_part = spread[:, :, 2 : tile_cols + 2]
    inner_part = inner_part.at[:, :, tile_cols - 2 : tile_cols].add(from_east)
    inner_part = inner_part.at[:, :, 0:2].add(from_west)
    lower_far_part = inner_part[:, 0:band_rows]
    lower_near_part = inner_part[:, band_rows : 2 * band_rows]
    owned = inner_part[:, 2 * band_rows : 3 * band_rows]
    upper_near_part = inner_part[:, 3 * band_rows : 4 * band_rows]
    upper_far_part = inner_part[:, 4 * band_rows : 5 * band_rows]
    owned = owned + passed_along(lower_near_part, "lat", -1)
    owned = owned + passed_along(lower_far_part, "lat", -2)
    owned = owned + passed_along(upper_near_part, "lat", 1)
    owned = owned + passed_along(upper_far_part, "lat", 2)
    adjoint_out = owned.astype(jnp.bfloat16).reshape(
        fields, levels, band_rows, tile_cols, cell_count
    )
    return (tangent_out, adjoint_out)


def solution(mesh):
    placed = (
        P("member", "lev", "lat", "lon", None),
        P("member", "lev", "lat", "lon", None),
        P("lat", "lon", None),
        P("lat", "lon", None),
        P("lat", "lon", None, None, None),
    )
    return jax.shard_map(
        on_device,
        mesh=mesh,
        in_specs=placed,
        out_specs=(P("member", "lev", "lat", "lon", None), P("member", "lev", "lat", "lon", None)),
        check_vma=False,
    )
```

profile of v0, /device:TPU:0, one launch (start us, length us, event | category | flops | bytes accessed | tf_op | source)
XLA Modules:
  0.0 115.9 jit_solution(1614947253521917316)
XLA Ops:
  2.3 1.8 %fusion.11 = f32[16,4,128,64]{2,3,1,0:T(8,128)S(1)} fusion(bf16[16,4,128,128]{3,2,1,0:T(8,128)(2,1)S(1)} %bitcast.33, bf16[64,16,128,1]{2,1,0,3:T(8,128)(2,1)} %bitcast.37), kind=kOutput, calls=%fused_computation.19 | convolution fusion | flops 134217728 | bytes 4456448 | tf_op jit(solution)/shard_map/rtc,tksc->rtks/dot_general | solution.py:77
  4.1 3.5 %convolution_bitcast_fusion = f32[64,20,8,128]{3,2,1,0:T(8,128)S(1)} fusion(f32[64,64,128]{2,0,1:T(8,128)S(1)} %bitcast.34, s32[64]{0:T(128)S(1)} %reshape.146), kind=kOutput, calls=%fused_computation.2 | convolution fusion | flops 1006643200 | bytes 7340288 | tf_op jit(solution)/shard_map/rms,mn->rns/dot_general | solution.py:84
  8.0 3.0 %collective-permute-start.6 = (bf16[64,20,2,128]{3,2,1,0:T(2,128)(2,1)S(1)}, bf16[64,20,2,128]{3,2,1,0:T(2,128)(2,1)S(1)}, u32[]{:S(2)}, u32[]{:S(2)}) collective-permute-start(bf16[64,20,2,128]{3,2,1,0:T(2,128)(2,1)S(1)} %slice.132), channel_id=1, source_target_pairs={{0,2},{2,0},{1,3},{3,1},{4,6},{6,4},{5,7},{7,5},{8,10},{10,8},{9,1... | collective-permute-start | bytes 1966088 | tf_op jit(solution)/shard_map/ppermute | solution.py:31
  11.8 5.2 %collective-permute-start = (bf16[2,32,4,4,128]{4,1,3,2,0:T(8,128)(2,1)}, bf16[2,32,4,4,128]{4,1,3,2,0:T(8,128)(2,1)}, u32[]{:S(2)}, u32[]{:S(2)}) collective-permute-start(bf16[2,32,4,4,128]{4,1,3,2,0:T(8,128)(2,1)} %copy.21), channel_id=1, source_target_pairs={{0,8},{4,12},{1,9},{5,13},{2,10},{6,14},{3,11},{7,15},{16,24},{20,... | collective-permute-start | bytes 786440 | tf_op jit(solution)/shard_map/ppermute | solution.py:10
  17.0 4.2 %collective-permute-start.1 = (bf16[2,32,4,4,128]{4,1,3,2,0:T(8,128)(2,1)}, bf16[2,32,4,4,128]{4,1,3,2,0:T(8,128)(2,1)}, u32[]{:S(2)}, u32[]{:S(2)}) collective-permute-start(bf16[2,32,4,4,128]{4,1,3,2,0:T(8,128)(2,1)} %copy.21), channel_id=1, source_target_pairs={{0,4},{4,8},{8,12},{1,5},{5,9},{9,13},{2,6},{6,10},{10,14},{3,7},{... | collective-permute-start | bytes 786440 | tf_op jit(solution)/shard_map/ppermute | solution.py:10
  21.2 1.3 %collective-permute-start.2 = (bf16[2,32,4,4,128]{4,1,3,2,0:T(8,128)(2,1)}, bf16[2,32,4,4,128]{4,1,3,2,0:T(8,128)(2,1)}, u32[]{:S(2)}, u32[]{:S(2)}) collective-permute-start(bf16[2,32,4,4,128]{4,1,3,2,0:T(8,128)(2,1)} %copy.21), channel_id=1, source_target_pairs={{4,0},{8,4},{12,8},{5,1},{9,5},{13,9},{6,2},{10,6},{14,10},{7,3},{... | collective-permute-start | bytes 786440 | tf_op jit(solution)/shard_map/ppermute | solution.py:10
  22.5 1.3 %collective-permute-start.3 = (bf16[2,32,4,4,128]{4,1,3,2,0:T(8,128)(2,1)}, bf16[2,32,4,4,128]{4,1,3,2,0:T(8,128)(2,1)}, u32[]{:S(2)}, u32[]{:S(2)}) collective-permute-start(bf16[2,32,4,4,128]{4,1,3,2,0:T(8,128)(2,1)} %copy.21), channel_id=1, source_target_pairs={{8,0},{12,4},{9,1},{13,5},{10,2},{14,6},{11,3},{15,7},{24,16},{28,... | collective-permute-start | bytes 786440 | tf_op jit(solution)/shard_map/ppermute | solution.py:10
  23.8 2.1 %slice.106 = f32[64,20,4,128]{3,2,1,0:T(4,128)} slice(f32[64,20,8,128]{3,2,1,0:T(8,128)S(1)} %convolution_bitcast_fusion), slice={[0:64], [0:20], [2:6], [0:128]} | slice | bytes 5242880 | tf_op jit(solution)/shard_map/slice | solution.py:88
  25.9 7.0 %fusion.20 = (f32[64,20,2,128]{3,2,1,0:T(2,128)}, f32[64,20,4,128]{3,2,1,0:T(4,128)}) fusion(f32[64,20,8,128]{3,2,1,0:T(8,128)} %copy-done.1, f32[64,20,4,128]{3,2,1,0:T(4,128)} %slice.106, bf16[64,20,2,128]{3,2,1,0:T(2,128)(2,1)S(1)} %collective-permute-done.6), kind=kLoop, calls=%fused_computation.40 | loop fusion | flops 655360 | bytes 5898240 | tf_op jit(solution)/shard_map/slice | solution.py:87
  33.0 1.6 %collective-permute-start.7 = (f32[64,20,2,128]{3,2,1,0:T(2,128)}, f32[64,20,2,128]{3,2,1,0:T(2,128)}, u32[]{:S(2)}, u32[]{:S(2)}) collective-permute-start(f32[64,20,2,128]{3,2,1,0:T(2,128)} %get-tuple-element.32), channel_id=1, source_target_pairs={{0,2},{2,0},{1,3},{3,1},{4,6},{6,4},{5,7},{7,5},{8,10},{10,8},{9,1... | collective-permute-start | bytes 3932168 | tf_op jit(solution)/shard_map/ppermute | solution.py:31
  38.8 2.0 %collective-permute-done.3 = bf16[2,32,4,4,128]{4,1,3,2,0:T(8,128)(2,1)} collective-permute-done((bf16[2,32,4,4,128]{4,1,3,2,0:T(8,128)(2,1)}, bf16[2,32,4,4,128]{4,1,3,2,0:T(8,128)(2,1)}, u32[]{:S(2)}, u32[]{:S(2)}) %collective-permute-start.3) | collective-permute-done | bytes 262176 | tf_op jit(solution)/shard_map/ppermute | solution.py:10
  45.0 19.9 %collective-permute-done.7 = f32[64,20,2,128]{3,2,1,0:T(2,128)} collective-permute-done((f32[64,20,2,128]{3,2,1,0:T(2,128)}, f32[64,20,2,128]{3,2,1,0:T(2,128)}, u32[]{:S(2)}, u32[]{:S(2)}) %collective-permute-start.7) | collective-permute-done | bytes 1310752 | tf_op jit(solution)/shard_map/ppermute | solution.py:31
  64.9 2.4 %fusion.1 = f32[64,20,4,128]{3,2,1,0:T(4,128)S(1)} fusion(f32[64,20,4,128]{3,2,1,0:T(4,128)S(1)} %copy-done.2, f32[64,20,2,128]{3,2,1,0:T(2,128)} %collective-permute-done.7), kind=kLoop, calls=%fused_computation.5 | loop fusion | flops 327680 | bytes 3932160 | tf_op jit(solution)/shard_map/scatter-add | solution.py:90
  67.4 1.8 %fusion.21 = (f32[64,4,4,128]{3,2,1,0:T(4,128)}, f32[64,4,4,128]{3,2,1,0:T(4,128)}, f32[64,4,4,128]{3,2,1,0:T(4,128)}, f32[64,4,4,128]{3,2,1,0:T(4,128)}) fusion(f32[64,20,4,128]{3,2,1,0:T(4,128)S(1)} %fusion.1), kind=kLoop, calls=%fused_computation.41 | loop fusion | bytes 4194304 | tf_op jit(solution)/shard_map/slice | solution.py:92
  69.6 5.3 %collective-permute-start.10 = (f32[64,4,4,128]{3,2,1,0:T(4,128)}, f32[64,4,4,128]{3,2,1,0:T(4,128)}, u32[]{:S(2)}, u32[]{:S(2)}) collective-permute-start(f32[64,4,4,128]{3,2,1,0:T(4,128)} %get-tuple-element.36), channel_id=1, source_target_pairs={{0,4},{4,8},{8,12},{1,5},{5,9},{9,13},{2,6},{6,10},{10,14},{3,7},{... | collective-permute-start | bytes 1572872 | tf_op jit(solution)/shard_map/ppermute | solution.py:10
  74.9 6.2 %collective-permute-start.11 = (f32[64,4,4,128]{3,2,1,0:T(4,128)}, f32[64,4,4,128]{3,2,1,0:T(4,128)}, u32[]{:S(2)}, u32[]{:S(2)}) collective-permute-start(f32[64,4,4,128]{3,2,1,0:T(4,128)} %get-tuple-element.35), channel_id=1, source_target_pairs={{0,8},{4,12},{1,9},{5,13},{2,10},{6,14},{3,11},{7,15},{16,24},{20,... | collective-permute-start | bytes 1572872 | tf_op jit(solution)/shard_map/ppermute | solution.py:10
  81.1 1.3 %collective-permute-start.8 = (f32[64,4,4,128]{3,2,1,0:T(4,128)}, f32[64,4,4,128]{3,2,1,0:T(4,128)}, u32[]{:S(2)}, u32[]{:S(2)}) collective-permute-start(f32[64,4,4,128]{3,2,1,0:T(4,128)} %get-tuple-element.34), channel_id=1, source_target_pairs={{4,0},{8,4},{12,8},{5,1},{9,5},{13,9},{6,2},{10,6},{14,10},{7,3},{... | collective-permute-start | bytes 1572872 | tf_op jit(solution)/shard_map/ppermute | solution.py:10
  82.4 1.3 %collective-permute-start.9 = (f32[64,4,4,128]{3,2,1,0:T(4,128)}, f32[64,4,4,128]{3,2,1,0:T(4,128)}, u32[]{:S(2)}, u32[]{:S(2)}) collective-permute-start(f32[64,4,4,128]{3,2,1,0:T(4,128)} %get-tuple-element.37), channel_id=1, source_target_pairs={{8,0},{12,4},{9,1},{13,5},{10,2},{14,6},{11,3},{15,7},{24,16},{28,... | collective-permute-start | bytes 1572872 | tf_op jit(solution)/shard_map/ppermute | solution.py:10
  83.8 7.3 %collective-permute-done.5 = bf16[2,32,20,2,128]{4,1,3,2,0:T(8,128)(2,1)} collective-permute-done((bf16[2,32,20,2,128]{4,1,3,2,0:T(8,128)(2,1)}, bf16[2,32,20,2,128]{4,1,3,2,0:T(8,128)(2,1)}, u32[]{:S(2)}, u32[]{:S(2)}) %collective-permute-start.5) | collective-permute-done | bytes 655392 | tf_op jit(solution)/shard_map/ppermute | solution.py:22
  91.2 1.6 %pad_maximum_fusion = bf16[2,32,20,8,128]{4,1,3,2,0:T(8,128)(2,1)S(1)} fusion(bf16[2,32,20,2,128]{4,1,3,2,0:T(8,128)(2,1)} %collective-permute-done.5, bf16[2,32,20,4,128]{4,1,3,2,0:T(8,128)(2,1)S(1)} %constant_dynamic-update-slice_fusion, bf16[2,32,20,2,128]{4,1,3,2,0:T(8,128)(2,1)} %collective-permute-done.4), kind=kLoop, calls=%fused_computation.1 | loop fusion | flops 2621440 | bytes 5242880 | tf_op jit(solution)/shard_map/concatenate | solution.py:18
  92.7 2.2 %copy.26 = bf16[2,32,20,8,128]{4,1,0,3,2:T(8,128)(2,1)} copy(bf16[2,32,20,8,128]{4,1,3,2,0:T(8,128)(2,1)S(1)} %pad_maximum_fusion) | data formatting | bytes 5242880 | tf_op jit(solution)/shard_map/concatenate | solution.py:18
  95.0 2.5 %gather_fusion = bf16[64,64,128]{2,1,0:T(8,128)(2,1)S(1)} fusion(bf16[64,160,128]{2,0,1:T(8,128)(2,1)} %bitcast.35, s32[1024]{0:T(1024)S(1)} %pad_clamp_fusion), kind=kCustom, calls=%fused_computation | custom fusion | bytes 2097408 | tf_op jit(solution)/shard_map/jit(_take)/gather | solution.py:68
  98.9 14.3 %collective-permute-done.9 = f32[64,4,4,128]{3,2,1,0:T(4,128)} collective-permute-done((f32[64,4,4,128]{3,2,1,0:T(4,128)}, f32[64,4,4,128]{3,2,1,0:T(4,128)}, u32[]{:S(2)}, u32[]{:S(2)}) %collective-permute-start.9) | collective-permute-done | bytes 524320 | tf_op jit(solution)/shard_map/ppermute | solution.py:10
  113.2 2.7 %fusion.9 = bf16[64,4,4,128]{3,2,1,0:T(4,128)(2,1)} fusion(f32[64,4,4,128]{3,2,1,0:T(4,128)} %collective-permute-done.11, f32[64,4,4,128]{3,2,1,0:T(4,128)} %collective-permute-done.10, f32[64,4,4,128]{3,2,1,0:T(4,128)} %collective-permute-done.9, f32[64,4,4,128]{3,2,1,0:T(4,128)} %collective-permute-done.8, f32[64,20,4,128]{3,2,1,0:T(4,128)} %copy-done.3), kind=kLoop, calls=%fused_computation.17 | loop fusion | flops 655360 | bytes 2883584 | tf_op jit(solution)/shard_map/convert_element_type | solution.py:100
  (38 shorter events, 13.2 us)
Async XLA Ops:
  0.6 1.6 %copy-start = (bf16[4,4,4,128,128]{4,3,2,1,0:T(8,128)(2,1)S(1)}, bf16[4,4,4,128,128]{4,3,2,1,0:T(8,128)(2,1)}, u32[]{:S(2)}) copy-start(bf16[4,4,4,128,128]{4,3,2,1,0:T(8,128)(2,1)} %param.13) | copy-start | bytes 6291460
  4.0 7.0 %copy-start.4 = (bf16[2,32,4,4,128]{4,3,2,1,0:T(4,128)(2,1)S(1)}, bf16[2,32,4,4,128]{4,3,2,1,0:T(4,128)(2,1)}, u32[]{:S(2)}) copy-start(bf16[2,32,4,4,128]{4,3,2,1,0:T(4,128)(2,1)} %param.9) | copy-start | bytes 786436
  7.6 18.2 %copy-start.1 = (f32[64,20,8,128]{3,2,1,0:T(8,128)}, f32[64,20,8,128]{3,2,1,0:T(8,128)S(1)}, u32[]{:S(2)}) copy-start(f32[64,20,8,128]{3,2,1,0:T(8,128)S(1)} %convolution_bitcast_fusion) | copy-start | bytes 15728644
  8.0 17.9 %collective-permute-start.6 = (bf16[64,20,2,128]{3,2,1,0:T(2,128)(2,1)S(1)}, bf16[64,20,2,128]{3,2,1,0:T(2,128)(2,1)S(1)}, u32[]{:S(2)}, u32[]{:S(2)}) collective-permute-start(bf16[64,20,2,128]{3,2,1,0:T(2,128)(2,1)S(1)} %slice.132), channel_id=1, source_target_pairs={{0,2},{2,0},{1,3},{3,1},{4,6},{6,4},{5,7},{7,5},{8,10},{10,8},{9,1... | collective-permute-start | bytes 1966088 | tf_op jit(solution)/shard_map/ppermute | solution.py:31
  11.8 22.8 %collective-permute-start = (bf16[2,32,4,4,128]{4,1,3,2,0:T(8,128)(2,1)}, bf16[2,32,4,4,128]{4,1,3,2,0:T(8,128)(2,1)}, u32[]{:S(2)}, u32[]{:S(2)}) collective-permute-start(bf16[2,32,4,4,128]{4,1,3,2,0:T(8,128)(2,1)} %copy.21), channel_id=1, source_target_pairs={{0,8},{4,12},{1,9},{5,13},{2,10},{6,14},{3,11},{7,15},{16,24},{20,... | collective-permute-start | bytes 786440 | tf_op jit(solution)/shard_map/ppermute | solution.py:10
  17.0 18.6 %collective-permute-start.1 = (bf16[2,32,4,4,128]{4,1,3,2,0:T(8,128)(2,1)}, bf16[2,32,4,4,128]{4,1,3,2,0:T(8,128)(2,1)}, u32[]{:S(2)}, u32[]{:S(2)}) collective-permute-start(bf16[2,32,4,4,128]{4,1,3,2,0:T(8,128)(2,1)} %copy.21), channel_id=1, source_target_pairs={{0,4},{4,8},{8,12},{1,5},{5,9},{9,13},{2,6},{6,10},{10,14},{3,7},{... | collective-permute-start | bytes 786440 | tf_op jit(solution)/shard_map/ppermute | solution.py:10
  21.2 16.7 %collective-permute-start.2 = (bf16[2,32,4,4,128]{4,1,3,2,0:T(8,128)(2,1)}, bf16[2,32,4,4,128]{4,1,3,2,0:T(8,128)(2,1)}, u32[]{:S(2)}, u32[]{:S(2)}) collective-permute-start(bf16[2,32,4,4,128]{4,1,3,2,0:T(8,128)(2,1)} %copy.21), channel_id=1, source_target_pairs={{4,0},{8,4},{12,8},{5,1},{9,5},{13,9},{6,2},{10,6},{14,10},{7,3},{... | collective-permute-start | bytes 786440 | tf_op jit(solution)/shard_map/ppermute | solution.py:10
  22.5 18.4 %collective-permute-start.3 = (bf16[2,32,4,4,128]{4,1,3,2,0:T(8,128)(2,1)}, bf16[2,32,4,4,128]{4,1,3,2,0:T(8,128)(2,1)}, u32[]{:S(2)}, u32[]{:S(2)}) collective-permute-start(bf16[2,32,4,4,128]{4,1,3,2,0:T(8,128)(2,1)} %copy.21), channel_id=1, source_target_pairs={{8,0},{12,4},{9,1},{13,5},{10,2},{14,6},{11,3},{15,7},{24,16},{28,... | collective-permute-start | bytes 786440 | tf_op jit(solution)/shard_map/ppermute | solution.py:10
  33.0 32.0 %collective-permute-start.7 = (f32[64,20,2,128]{3,2,1,0:T(2,128)}, f32[64,20,2,128]{3,2,1,0:T(2,128)}, u32[]{:S(2)}, u32[]{:S(2)}) collective-permute-start(f32[64,20,2,128]{3,2,1,0:T(2,128)} %get-tuple-element.32), channel_id=1, source_target_pairs={{0,2},{2,0},{1,3},{3,1},{4,6},{6,4},{5,7},{7,5},{8,10},{10,8},{9,1... | collective-permute-start | bytes 3932168 | tf_op jit(solution)/shard_map/ppermute | solution.py:31
  36.6 28.3 %copy-start.2 = (f32[64,20,4,128]{3,2,1,0:T(4,128)S(1)}, f32[64,20,4,128]{3,2,1,0:T(4,128)}, u32[]{:S(2)}) copy-start(f32[64,20,4,128]{3,2,1,0:T(4,128)} %get-tuple-element.33) | copy-start | bytes 7864324
  43.0 39.4 %collective-permute-start.4 = (bf16[2,32,20,2,128]{4,1,3,2,0:T(8,128)(2,1)S(1)}, bf16[2,32,20,2,128]{4,1,3,2,0:T(8,128)(2,1)}, u32[]{:S(2)}, u32[]{:S(2)}) collective-permute-start(bf16[2,32,20,2,128]{4,1,3,2,0:T(8,128)(2,1)S(1)} %get-tuple-element.38), channel_id=1, source_target_pairs={{0,2},{2,0},{1,3},{3,1},{4,6},{6,4},{5,7},{7,5},{8,10},{10,8},{9,1... | collective-permute-start | bytes 1966088 | tf_op jit(solution)/shard_map/ppermute | solution.py:20
  44.0 47.2 %collective-permute-start.5 = (bf16[2,32,20,2,128]{4,1,3,2,0:T(8,128)(2,1)}, bf16[2,32,20,2,128]{4,1,3,2,0:T(8,128)(2,1)}, u32[]{:S(2)}, u32[]{:S(2)}) collective-permute-start(bf16[2,32,20,2,128]{4,1,3,2,0:T(8,128)(2,1)} %get-tuple-element.39), channel_id=1, source_target_pairs={{2,0},{0,2},{3,1},{1,3},{6,4},{4,6},{7,5},{5,7},{10,8},{8,10},{11,... | collective-permute-start | bytes 1966088 | tf_op jit(solution)/shard_map/ppermute | solution.py:22
  67.4 2.2 %copy-start.3 = (f32[64,20,4,128]{3,2,1,0:T(4,128)}, f32[64,20,4,128]{3,2,1,0:T(4,128)S(1)}, u32[]{:S(2)}) copy-start(f32[64,20,4,128]{3,2,1,0:T(4,128)S(1)} %fusion.1) | copy-start | bytes 7864324
  69.6 29.3 %collective-permute-start.10 = (f32[64,4,4,128]{3,2,1,0:T(4,128)}, f32[64,4,4,128]{3,2,1,0:T(4,128)}, u32[]{:S(2)}, u32[]{:S(2)}) collective-permute-start(f32[64,4,4,128]{3,2,1,0:T(4,128)} %get-tuple-element.36), channel_id=1, source_target_pairs={{0,4},{4,8},{8,12},{1,5},{5,9},{9,13},{2,6},{6,10},{10,14},{3,7},{... | collective-permute-start | bytes 1572872 | tf_op jit(solution)/shard_map/ppermute | solution.py:10
  74.9 24.0 %collective-permute-start.11 = (f32[64,4,4,128]{3,2,1,0:T(4,128)}, f32[64,4,4,128]{3,2,1,0:T(4,128)}, u32[]{:S(2)}, u32[]{:S(2)}) collective-permute-start(f32[64,4,4,128]{3,2,1,0:T(4,128)} %get-tuple-element.35), channel_id=1, source_target_pairs={{0,8},{4,12},{1,9},{5,13},{2,10},{6,14},{3,11},{7,15},{16,24},{20,... | collective-permute-start | bytes 1572872 | tf_op jit(solution)/shard_map/ppermute | solution.py:10
  81.1 17.8 %collective-permute-start.8 = (f32[64,4,4,128]{3,2,1,0:T(4,128)}, f32[64,4,4,128]{3,2,1,0:T(4,128)}, u32[]{:S(2)}, u32[]{:S(2)}) collective-permute-start(f32[64,4,4,128]{3,2,1,0:T(4,128)} %get-tuple-element.34), channel_id=1, source_target_pairs={{4,0},{8,4},{12,8},{5,1},{9,5},{13,9},{6,2},{10,6},{14,10},{7,3},{... | collective-permute-start | bytes 1572872 | tf_op jit(solution)/shard_map/ppermute | solution.py:10
  82.4 30.8 %collective-permute-start.9 = (f32[64,4,4,128]{3,2,1,0:T(4,128)}, f32[64,4,4,128]{3,2,1,0:T(4,128)}, u32[]{:S(2)}, u32[]{:S(2)}) collective-permute-start(f32[64,4,4,128]{3,2,1,0:T(4,128)} %get-tuple-element.37), channel_id=1, source_target_pairs={{8,0},{12,4},{9,1},{13,5},{10,2},{14,6},{11,3},{15,7},{24,16},{28,... | collective-permute-start | bytes 1572872 | tf_op jit(solution)/shard_map/ppermute | solution.py:10
where the time goes:
time: 117 us; the launch traced here: 116 us
  waiting for transfers between devices  43.6 us (37%)
  starting transfers between devices  32.7 us (28%)
  local copies, waits for them, and re-layouts  18.3 us (16%)
  other arithmetic  14.7 us (13%)
  matrix products  5.84 us (5%)
    ppermute x8, starting transfers between devices, passed_along(): return lax.ppermute(array, axis, pairs)  26 us
    ppermute x2, waiting for transfers between devices, shifted(): lax.ppermute(array, axis, [(i, (i + by) % devices) for i in range(devices)])  19.9 us
    ppermute x8, waiting for transfers between devices, passed_along(): return lax.ppermute(array, axis, pairs)  16.3 us
    ppermute x1, waiting for transfers between devices, padded(): lax.ppermute(head, axis, [((i + 1) % count, i) for i in range(count)])  7.33 us
    slice x1, other arithmetic, on_device(): from_west = shifted(spread[:, :, span_cols - 2:span_cols], 'lon', 1)  7.04 us
    unnamed x16, local copies, waits for them, and re-layouts  6.89 us
    ppermute x2, starting transfers between devices, shifted(): lax.ppermute(array, axis, [(i, (i + by) % devices) for i in range(devices)])  4.63 us
    dot_general x1, matrix products, on_device(): jnp.einsum('rms,mn->rns', contributions, onehot, precision=lax.Precision....  3.55 us
  transfers between devices with their start and end apart: 12, of which 4 were waited for; matrix products, arithmetic and copies ran while one was open for 24% of the time, Pallas kernels for 0%

commit v1 on v0

v1 whole, which is shorter than its diff:
```python
import functools
import jax
import jax.numpy as jnp
from jax import lax
from jax.experimental import pallas as pl
from jax.experimental.pallas import tpu as pltpu
from jax.sharding import PartitionSpec as P

POLAR_ROWS = 4
REACH = 2
HALO = 2
BANDS = 2 * REACH + 1
MESH = pl.DeviceIdType.MESH


def exchange(
    sizes,
    where_ref, own_ref, forcing_ref, onehot_ref, weights,
    tangent_ref, adjoint_ref,
    ext, contrib, spread, x_out, x_in, far_out, far_in, near_out, near_in,
    own_sem, z_send, z_recv, x_send, x_recv, ax_send, ax_recv, az_send, az_recv,
):
    lat_count, lon_count, rows, cols, stencil = sizes
    depth, cells = own_ref.shape[1], own_ref.shape[2]
    span = cols + 2 * HALO
    tile = rows * cols
    targets = tile
    picks = targets * stencil
    places = BANDS * span * rows
    half = cols // 2
    z = lax.axis_index("lat")
    x = lax.axis_index("lon")
    west = lax.rem(x + lon_count - 1, lon_count)
    east = lax.rem(x + 1, lon_count)
    polar = (z * rows < POLAR_ROWS) | ((z + 1) * rows > lat_count * rows - POLAR_ROWS)
    sides = ({"lon": west}, {"lon": east})
    steps = (1, -1)

    def there(offset):
        return (z + offset >= 0) & (z + offset < lat_count)

    def place(band, column):
        return ((band + REACH) * span + column) * rows

    barrier = pltpu.get_barrier_semaphore()
    for side in sides:
        pl.semaphore_signal(barrier, inc=1, device_id=side, device_id_type=MESH)
    for step in steps:
        @pl.when(there(step))
        def _():
            pl.semaphore_signal(barrier, inc=1, device_id={"lat": z + step}, device_id_type=MESH)

    own_copy = pltpu.make_async_copy(
        own_ref, ext.at[pl.ds(place(0, HALO), tile)], own_sem
    )
    own_copy.start()
    peers = len(sides) + (2 if lat_count > 2 else lat_count - 1)
    inner = there(1) & there(-1)

    @pl.when(inner)
    def _():
        pl.semaphore_wait(barrier, peers)

    @pl.when(jnp.logical_not(inner))
    def _():
        pl.semaphore_wait(barrier, peers - 1 if lat_count > 2 else peers)

    def z_copy(d, hop, part):
        source_band = -steps[d] if hop else 0
        band = -steps[d] * (hop + 1)
        offset = part * half
        size = half * rows
        if hop:
            src = ext.at[pl.ds(place(source_band, HALO + offset), size)]
        else:
            src = own_ref.at[pl.ds(offset * rows, size)]
        return pltpu.make_async_remote_copy(
            src_ref=src,
            dst_ref=ext.at[pl.ds(place(band, HALO + offset), size)],
            send_sem=z_send.at[d, hop, part],
            recv_sem=z_recv.at[d, hop, part],
            device_id={"lat": z + steps[d]},
            device_id_type=MESH,
        )

    def x_copy(band, side, j):
        mine = j if side == 0 else cols - 1 - j
        lands = cols + HALO + j if side == 0 else HALO - 1 - j
        if band == 0:
            src = own_ref.at[pl.ds(mine * rows, rows)]
        else:
            src = ext.at[pl.ds(place(band, HALO + mine), rows)]
        return pltpu.make_async_remote_copy(
            src_ref=src,
            dst_ref=ext.at[pl.ds(place(band, lands), rows)],
            send_sem=x_send.at[band + REACH, side, j],
            recv_sem=x_recv.at[band + REACH, side, j],
            device_id=sides[side],
            device_id_type=MESH,
        )

    def ax_copy(band, side, j):
        return pltpu.make_async_remote_copy(
            src_ref=x_out.at[band + REACH, side, j],
            dst_ref=x_in.at[band + REACH, side, j],
            send_sem=ax_send.at[band + REACH, side, j],
            recv_sem=ax_recv.at[band + REACH, side, j],
            device_id=sides[side],
            device_id_type=MESH,
        )

    def az_copy(d, near):
        return pltpu.make_async_remote_copy(
            src_ref=(near_out if near else far_out).at[d],
            dst_ref=(near_in if near else far_in).at[d],
            send_sem=az_send.at[d, near],
            recv_sem=az_recv.at[d, near],
            device_id={"lat": z + steps[d]},
            device_id_type=MESH,
        )

    def x_all(make, band, act):
        @pl.when(there(band))
        def _():
            for side in range(2):
                act(make(band, side, 0), band, side, 0)

            @pl.when(polar)
            def _():
                for side in range(2):
                    act(make(band, side, 1), band, side, 1)

    def start(copy, *_):
        copy.start()

    def wait_send(copy, *_):
        copy.wait_send()

    def wait_recv(copy, *_):
        copy.wait_recv()

    for d in range(2):
        @pl.when(there(steps[d]))
        def _():
            for part in range(2):
                z_copy(d, 0, part).start()
    x_all(x_copy, 0, start)

    def contribute(t, carry):
        block = weights[pl.ds(t * stencil, stencil)].reshape(stencil * cells, cells)
        part = lax.dot_general(
            forcing_ref[t], block, (((1,), (1,)), ((), ())), preferred_element_type=jnp.float32
        )
        for k in range(stencil):
            first = pl.multiple_of((t * stencil + k) * depth, depth)
            contrib[pl.ds(first, depth), :] = part[:, k * cells : (k + 1) * cells]
        return carry

    lax.fori_loop(0, targets, contribute, 0, unroll=2)

    def spread_rows(pair, carry):
        pieces = []
        for i in range(2):
            value = contrib[pl.ds(pair * 2 + i, picks, stride=depth), :]
            high = value.astype(jnp.bfloat16)
            low = (value - high.astype(jnp.float32)).astype(jnp.bfloat16)
            pieces.append(jnp.concatenate([high, low], axis=0))
        summed = jnp.dot(
            onehot_ref[...],
            jnp.concatenate(pieces, axis=1),
            preferred_element_type=jnp.float32,
        )
        for i in range(2):
            spread[pl.ds(pair * 2 + i, places, stride=depth), :] = summed[
                :, i * cells : (i + 1) * cells
            ]
        return carry

    lax.fori_loop(0, depth // 2, spread_rows, 0, unroll=2)

    def at(first, count):
        return pl.ds(first * depth, count * depth)

    def ax_start(copy, band, side, j):
        column = HALO - 1 - j if side == 0 else HALO + cols + j
        value = spread[at(place(band, column), rows), :].astype(jnp.bfloat16)
        x_out[band + REACH, side, j] = value.reshape(rows, depth, cells)
        copy.start()

    def ax_finish(copy, band, side, j):
        copy.wait_recv()
        column = HALO + cols - 1 - j if side == 0 else HALO + j
        here = at(place(band, column), rows)
        value = x_in[band + REACH, side, j].astype(jnp.float32)
        spread[here, :] += value.reshape(rows * depth, cells)

    for band in (2, -2):
        x_all(ax_copy, band, ax_start)
    for d in range(2):
        @pl.when(there(-steps[d]))
        def _():
            for part in range(2):
                z_copy(d, 0, part).wait_recv()

                @pl.when(there(steps[d]))
                def _():
                    z_copy(d, 1, part).start()
        x_all(x_copy, -steps[d], start)
    for band in (1, -1):
        x_all(ax_copy, band, ax_start)
    for d in range(2):
        @pl.when(there(-2 * steps[d]))
        def _():
            for part in range(2):
                z_copy(d, 1, part).wait_recv()
        x_all(x_copy, -2 * steps[d], start)
    x_all(ax_copy, 0, ax_start)

    for d in range(2):
        x_all(ax_copy, 2 * steps[d], ax_finish)

        @pl.when(there(2 * steps[d]))
        def _():
            value = spread[at(place(2 * steps[d], HALO), tile), :].astype(jnp.bfloat16)
            far_out[d] = value.reshape(tile, depth, cells)
            az_copy(d, 0).start()
    for d in range(2):
        x_all(ax_copy, steps[d], ax_finish)

        @pl.when(there(steps[d]))
        def _():
            here = at(place(steps[d], HALO), tile)

            @pl.when(there(-steps[d]))
            def _():
                az_copy(d, 0).wait_recv()
                spread[here, :] += far_in[d].astype(jnp.float32).reshape(tile * depth, cells)

            near_out[d] = spread[here, :].astype(jnp.bfloat16).reshape(tile, depth, cells)
            az_copy(d, 1).start()

    own_copy.wait()
    for band in range(-REACH, REACH + 1):
        x_all(x_copy, band, wait_recv)

    def interpolate(t, carry):
        sources = [ext[where_ref[t * stencil + k]] for k in range(stencil)]
        block = weights[pl.ds(t * stencil, stencil)].reshape(stencil * cells, cells)
        value = jnp.dot(
            jnp.concatenate(sources, axis=1), block, preferred_element_type=jnp.float32
        )
        tangent_ref[t] = value.astype(jnp.bfloat16)
        return carry

    lax.fori_loop(0, targets, interpolate, 0, unroll=2)

    x_all(ax_copy, 0, ax_finish)
    here = at(place(0, HALO), tile)
    for d in range(2):
        @pl.when(there(-steps[d]))
        def _():
            az_copy(d, 1).wait_recv()
            spread[here, :] += near_in[d].astype(jnp.float32).reshape(tile * depth, cells)
    adjoint_ref[...] = spread[here, :].astype(jnp.bfloat16).reshape(tile, depth, cells)

    for band in range(-REACH, REACH + 1):
        x_all(x_copy, band, wait_send)
        x_all(ax_copy, band, wait_send)
    for d in range(2):
        @pl.when(there(steps[d]))
        def _():
            for part in range(2):
                z_copy(d, 0, part).wait_send()
            az_copy(d, 1).wait_send()

            @pl.when(there(-steps[d]))
            def _():
                for part in range(2):
                    z_copy(d, 1, part).wait_send()

        @pl.when(there(2 * steps[d]))
        def _():
            az_copy(d, 0).wait_send()


def on_device(perturbation, adjoint_forcing, source_rows, source_cols, cubic_weights):
    fields, levels, rows, cols, cells = perturbation.shape
    stencil = source_rows.shape[2]
    depth = fields * levels
    span = cols + 2 * HALO
    tile = rows * cols
    picks = tile * stencil
    places = BANDS * span * rows
    lat_count = lax.axis_size("lat")
    lon_count = lax.axis_size("lon")
    z = lax.axis_index("lat")
    x = lax.axis_index("lon")
    local_rows = source_rows - z * rows + REACH * rows
    local_cols = jnp.mod(source_cols - x * cols + HALO, cols * lon_count)
    where = ((local_rows // rows) * span + local_cols) * rows + local_rows % rows
    where = where.reshape(picks).astype(jnp.int32)
    onehot = jnp.arange(places, dtype=jnp.int32)[:, None] == jnp.tile(where, 2)[None, :]
    onehot = onehot.astype(jnp.bfloat16)
    own = perturbation.transpose(3, 2, 0, 1, 4).reshape(tile, depth, cells)
    forcing = adjoint_forcing.transpose(2, 3, 0, 1, 4).reshape(tile, depth, cells)
    weights = cubic_weights.reshape(picks, cells, cells)

    vmem = pl.BlockSpec(memory_space=pltpu.VMEM)
    dma = pltpu.SemaphoreType.DMA
    bf16, f32 = jnp.bfloat16, jnp.float32
    tangent, adjoint = pl.pallas_call(
        functools.partial(exchange, (lat_count, lon_count, rows, cols, stencil)),
        name="exchange",
        out_shape=(
            jax.ShapeDtypeStruct((tile, depth, cells), bf16),
            jax.ShapeDtypeStruct((tile, depth, cells), bf16),
        ),
        in_specs=[
            pl.BlockSpec(memory_space=pltpu.SMEM),
            vmem,
            vmem,
            vmem,
            vmem,
        ],
        out_specs=(vmem, vmem),
        scratch_shapes=[
            pltpu.VMEM((places, depth, cells), bf16),
            pltpu.VMEM((picks * depth, cells), f32),
            pltpu.VMEM((places * depth, cells), f32),
            pltpu.VMEM((BANDS, 2, 2, rows, depth, cells), bf16),
            pltpu.VMEM((BANDS, 2, 2, rows, depth, cells), bf16),
            pltpu.VMEM((2, tile, depth, cells), bf16),
            pltpu.VMEM((2, tile, depth, cells), bf16),
            pltpu.VMEM((2, tile, depth, cells), bf16),
            pltpu.VMEM((2, tile, depth, cells), bf16),
            dma,
            dma((2, 2, 2)),
            dma((2, 2, 2)),
            dma((BANDS, 2, 2)),
            dma((BANDS, 2, 2)),
            dma((BANDS, 2, 2)),
            dma((BANDS, 2, 2)),
            dma((2, 2)),
            dma((2, 2)),
        ],
        compiler_params=pltpu.CompilerParams(
            collective_id=0, has_side_effects=True, vmem_limit_bytes=48 * 1024 * 1024
        ),
    )(where, own, forcing, onehot, weights)

    tangent_out = tangent.reshape(rows, cols, fields, levels, cells).transpose(2, 3, 0, 1, 4)
    adjoint_out = adjoint.reshape(cols, rows, fields, levels, cells).transpose(2, 3, 1, 0, 4)
    return (tangent_out, adjoint_out)


def solution(mesh):
    placed = (
        P("member", "lev", "lat", "lon", None),
        P("member", "lev", "lat", "lon", None),
        P("lat", "lon", None),
        P("lat", "lon", None),
        P("lat", "lon", None, None, None),
    )
    return jax.shard_map(
        on_device,
        mesh=mesh,
        in_specs=placed,
        out_specs=(P("member", "lev", "lat", "lon", None), P("member", "lev", "lat", "lon", None)),
        check_vma=False,
    )
```

time: 117 us -> 50.1 us (0.43)
  waiting for transfers between devices: 43.6 us -> 0 us
  Pallas kernels: 0 us -> 42.8 us
  starting transfers between devices: 32.7 us -> 0 us
  other arithmetic: 14.7 us -> 0.77 us
  local copies, waits for them, and re-layouts: 18.3 us -> 5.62 us
  matrix products: 5.84 us -> 0 us
    ppermute x12 -> x0, waiting for transfers between devices: 43.6 us -> none  [the longest x2 19.9 us: shifted(): lax.ppermute(array, axis, [(i, (i + by) % devices) for i in range(devices)])]
    pallas_call x0 -> x1, Pallas kernels: none -> 42.8 us  [on_device(): pl.pallas_call(functools.partial(exchange, (lat_count, lon_count, rows, c...]
    ppermute x12 -> x0, starting transfers between devices: 32.7 us -> none  [the longest x8 26 us: passed_along(): return lax.ppermute(array, axis, pairs)]
    slice x1 -> x0, other arithmetic: 7.04 us -> none  [on_device(): from_west = shifted(spread[:, :, span_cols - 2:span_cols], 'lon', 1)]
    dot_general x3 -> x0, matrix products: 5.84 us -> none  [the longest x1 3.55 us: on_device(): jnp.einsum('rms,mn->rns', contributions, onehot, precision=lax.Precision....]
    slice x4 -> x0, local copies, waits for them, and re-layouts: 5.37 us -> none  [the longest x1 2.08 us: on_device(): inner_part = spread[:, :, 2:tile_cols + 2]]
    unnamed x16 -> x2, local copies, waits for them, and re-layouts: 6.89 us -> 1.59 us
    concatenate x2 -> x0, local copies, waits for them, and re-layouts: 3.22 us -> none  [the longest x1 2.23 us: padded(): jnp.concatenate([lax.ppermute(tail, axis, [(i, (i + 1) % count) for i in...]
  transfers between devices with their start and end apart: 12 -> 0, of which waited for: 4 -> 0; matrix products, arithmetic and copies ran while one was open for 24% -> 0% of each run, Pallas kernels for 0% -> 0%
where the time goes in v1:
time: 50.1 us; the launch traced here: 49.9 us
  Pallas kernels  42.8 us (85%)
  local copies, waits for them, and re-layouts  5.62 us (11%)
  other arithmetic  0.77 us (2%)
  between operations  0.68 us (1%)
    pallas_call x1, Pallas kernels, on_device(): pl.pallas_call(functools.partial(exchange, (lat_count, lon_count, rows, c...  42.8 us
    unnamed x2, local copies, waits for them, and re-layouts  1.59 us
    transpose x1, local copies, waits for them, and re-layouts, on_device(): own = perturbation.transpose(3, 2, 0, 1, 4).reshape(tile, depth, cells)  1.02 us
    transpose x1, local copies, waits for them, and re-layouts, on_device(): adjoint_forcing.transpose(2, 3, 0, 1, 4).reshape(tile, depth, cells)  1.02 us

profile of v1, /device:TPU:0, one launch (start us, length us, event | category | flops | bytes accessed | tf_op | source)
XLA Modules:
  0.0 49.9 jit_solution(6440190057047479403)
XLA Ops:
  0.6 0.7 %fusion.4 = s32[4,4,4]{2,1,0:T(4,128)S(1)} fusion(s32[4,4,4]{2,1,0:T(4,128)} %param.7, s32[4,4,4]{2,1,0:T(4,128)} %param.8, s32[]{:T(128)S(6)} %mul.15, s32[]{:T(128)S(6)} %mul.13), kind=kLoop, calls=%fused_computation.15 | loop fusion | flops 2432 | bytes 776 | tf_op jit(solution)/shard_map/add | solution.py:300
  1.4 0.1 reshape.24.where_ref
  1.5 0.1 eq.19
  1.6 1.0 %copy.7 = bf16[4,4,2,32,128]{4,3,2,1,0:T(8,128)(2,1)S(1)} copy(bf16[4,4,2,32,128]{4,0,1,3,2:T(4,128)(2,1)} %bitcast.18) | data formatting | bytes 524288 | tf_op jit(solution)/shard_map/transpose | solution.py:304
  2.6 1.0 %copy.8 = bf16[4,4,2,32,128]{4,3,2,1,0:T(8,128)(2,1)S(1)} copy(bf16[4,4,2,32,128]{4,1,0,3,2:T(4,128)(2,1)} %bitcast.19) | data formatting | bytes 524288 | tf_op jit(solution)/shard_map/transpose | solution.py:305
  3.6 0.0 copy-start
  3.7 1.6 %copy-done = bf16[4,4,4,128,128]{4,3,2,1,0:T(8,128)(2,1)S(1)} copy-done((bf16[4,4,4,128,128]{4,3,2,1,0:T(8,128)(2,1)S(1)}, bf16[4,4,4,128,128]{4,3,2,1,0:T(8,128)(2,1)}, u32[]{:S(2)}) %copy-start) | copy-done | bytes 2097176
  5.2 42.8 %exchange.1 = (bf16[16,64,128]{2,1,0:T(8,128)(2,1)S(1)}, bf16[16,64,128]{2,1,0:T(8,128)(2,1)S(1)}) custom-call(s32[64]{0:T(128)S(1)} %reshape.24.where_ref, bf16[16,64,128]{2,1,0:T(8,128)(2,1)S(1)} %bitcast.14, bf16[16,64,128]{2,1,0:T(8,128)(2,1)S(1)} %bitcast.15, bf16[160,128]{1,0:T(8,128)(2,1)S(1)} %fusion.onehot_ref, bf16[64,128,128]{2,1,0:T(8,128)(2,1)S(1)} %bitcast.13), custom_call_target="tpu_custom_call" | custom-call | tf_op jit(solution)/shard_map/exchange/pallas_call | solution.py:311
  48.1 0.9 %copy.14 = bf16[4,4,2,32,128]{4,1,0,3,2:T(4,128)(2,1)} copy(bf16[4,4,2,32,128]{4,3,2,1,0:T(8,128)(2,1)S(1)} %bitcast.17) | data formatting | bytes 524288 | tf_op jit(solution)/shard_map/reshape | solution.py:351
  49.0 0.9 %copy.13 = bf16[4,4,2,32,128]{4,0,1,3,2:T(4,128)(2,1)} copy(bf16[4,4,2,32,128]{4,3,2,1,0:T(8,128)(2,1)S(1)} %bitcast.16) | data formatting | bytes 524288 | tf_op jit(solution)/shard_map/reshape | solution.py:352
  (2 shorter events, 0.0 us)
Async XLA Ops:
  3.6 1.6 %copy-start = (bf16[4,4,4,128,128]{4,3,2,1,0:T(8,128)(2,1)S(1)}, bf16[4,4,4,128,128]{4,3,2,1,0:T(8,128)(2,1)}, u32[]{:S(2)}) copy-start(bf16[4,4,4,128,128]{4,3,2,1,0:T(8,128)(2,1)} %param.9) | copy-start | bytes 6291460

commit v2 on v1

--- a/solution.py
+++ b/solution.py
@@ -15,10 +15,10 @@
 
 def exchange(
     sizes,
-    where_ref, own_ref, forcing_ref, onehot_ref, weights,
+    where_ref, own_ref, forcing_ref, onehot_ref, weights_hbm,
     tangent_ref, adjoint_ref,
-    ext, contrib, spread, x_out, x_in, far_out, far_in, near_out, near_in,
-    own_sem, z_send, z_recv, x_send, x_recv, ax_send, ax_recv, az_send, az_recv,
+    ext, weights, contrib, spread, x_out, x_in, lent, far_out, far_in, near_out, near_in,
+    weight_sem, own_sem, fwd_send, fwd_recv, lend_send, lend_recv, z_send, z_recv, x_send, x_recv, ax_send, ax_recv, az_send, az_recv,
 ):
     lat_count, lon_count, rows, cols, stencil = sizes
     depth, cells = own_ref.shape[1], own_ref.shape[2]
@@ -50,6 +50,8 @@
         def _():
             pl.semaphore_signal(barrier, inc=1, device_id={"lat": z + step}, device_id_type=MESH)
 
+    weight_copy = pltpu.make_async_copy(weights_hbm, weights, weight_sem)
+    weight_copy.start()
     own_copy = pltpu.make_async_copy(
         own_ref, ext.at[pl.ds(place(0, HALO), tile)], own_sem
     )
@@ -119,16 +121,47 @@
             device_id_type=MESH,
         )
 
-    def x_all(make, band, act):
+    lending = lat_count >= 4
+    poles = ((0, 1), (lat_count - 1, -1)) if lending else ()
+
+    def fwd_copy(pole, step, i, side):
+        column = HALO + cols if side == 0 else HALO - 1
+        return pltpu.make_async_remote_copy(
+            src_ref=ext.at[pl.ds(place(i * step, column), rows)],
+            dst_ref=ext.at[pl.ds(place((i + 1) * step, column), rows)],
+            send_sem=fwd_send.at[i, side],
+            recv_sem=fwd_recv.at[i, side],
+            device_id={"lat": pole},
+            device_id_type=MESH,
+        )
+
+    def lend_copy(pole, step, i, side):
+        return pltpu.make_async_remote_copy(
+            src_ref=x_out.at[(i + 1) * step + REACH, side, 0],
+            dst_ref=lent.at[i, side],
+            send_sem=lend_send.at[i, side],
+            recv_sem=lend_recv.at[i, side],
+            device_id={"lat": pole + step},
+            device_id_type=MESH,
+        )
+
+    def x_all(make, band, act, which=(0, 1)):
         @pl.when(there(band))
         def _():
-            for side in range(2):
-                act(make(band, side, 0), band, side, 0)
-
-            @pl.when(polar)
-            def _():
+            def edge():
                 for side in range(2):
-                    act(make(band, side, 1), band, side, 1)
+                    act(make(band, side, 0), band, side, 0)
+
+            if 0 in which:
+                if band != 0 and lending:
+                    pl.when(jnp.logical_not(polar))(edge)
+                else:
+                    edge()
+            if 1 in which:
+                @pl.when(polar)
+                def _():
+                    for side in range(2):
+                        act(make(band, side, 1), band, side, 1)
 
     def start(copy, *_):
         copy.start()
@@ -145,6 +178,8 @@
             for part in range(2):
                 z_copy(d, 0, part).start()
     x_all(x_copy, 0, start)
+
+    weight_copy.wait()
 
     def contribute(t, carry):
         block = weights[pl.ds(t * stencil, stencil)].reshape(stencil * cells, cells)
@@ -181,9 +216,11 @@
     def at(first, count):
         return pl.ds(first * depth, count * depth)
 
+    def away(side, j):
+        return HALO - 1 - j if side == 0 else HALO + cols + j
+
     def ax_start(copy, band, side, j):
-        column = HALO - 1 - j if side == 0 else HALO + cols + j
-        value = spread[at(place(band, column), rows), :].astype(jnp.bfloat16)
+        value = spread[at(place(band, away(side, j)), rows), :].astype(jnp.bfloat16)
         x_out[band + REACH, side, j] = value.reshape(rows, depth, cells)
         copy.start()
 
@@ -194,6 +231,12 @@
         value = x_in[band + REACH, side, j].astype(jnp.float32)
         spread[here, :] += value.reshape(rows * depth, cells)
 
+    for pole, step in poles:
+        @pl.when(z == pole)
+        def _():
+            for i in range(2):
+                for side in range(2):
+                    ax_start(lend_copy(pole, step, i, side), (i + 1) * step, side, 0)
     for band in (2, -2):
         x_all(ax_copy, band, ax_start)
     for d in range(2):
@@ -206,6 +249,18 @@
                 def _():
                     z_copy(d, 1, part).start()
         x_all(x_copy, -steps[d], start)
+    x_all(x_copy, 0, wait_recv, (0,))
+    for pole, step in poles:
+        @pl.when(z == pole + step)
+        def _():
+            for side in range(2):
+                fwd_copy(pole, step, 0, side).start()
+            for i in range(2):
+                for side in range(2):
+                    lend_copy(pole, step, i, side).wait_recv()
+                    here = at(place(i * step, away(side, 0)), rows)
+                    value = lent[i, side].astype(jnp.float32)
+                    spread[here, :] += value.reshape(rows * depth, cells)
     for band in (1, -1):
         x_all(ax_copy, band, ax_start)
     for d in range(2):
@@ -215,6 +270,13 @@
                 z_copy(d, 1, part).wait_recv()
         x_all(x_copy, -2 * steps[d], start)
     x_all(ax_copy, 0, ax_start)
+    for band in (1, -1):
+        x_all(x_copy, band, wait_recv, (0,))
+    for pole, step in poles:
+        @pl.when(z == pole + step)
+        def _():
+            for side in range(2):
+                fwd_copy(pole, step, 1, side).start()
 
     for d in range(2):
         x_all(ax_copy, 2 * steps[d], ax_finish)
@@ -241,7 +303,13 @@
 
     own_copy.wait()
     for band in range(-REACH, REACH + 1):
-        x_all(x_copy, band, wait_recv)
+        x_all(x_copy, band, wait_recv, (0, 1) if abs(band) == 2 else (1,))
+    for pole, step in poles:
+        @pl.when(z == pole)
+        def _():
+            for i in range(2):
+                for side in range(2):
+                    fwd_copy(pole, step, i, side).wait_recv()
 
     def interpolate(t, carry):
         sources = [ext[where_ref[t * stencil + k]] for k in range(stencil)]
@@ -266,6 +334,16 @@
     for band in range(-REACH, REACH + 1):
         x_all(x_copy, band, wait_send)
         x_all(ax_copy, band, wait_send)
+    for pole, step in poles:
+        for i in range(2):
+            for side in range(2):
+                @pl.when(z == pole)
+                def _():
+                    lend_copy(pole, step, i, side).wait_send()
+
+                @pl.when(z == pole + step)
+                def _():
+                    fwd_copy(pole, step, i, side).wait_send()
     for d in range(2):
         @pl.when(there(steps[d]))
         def _():
@@ -320,20 +398,27 @@
             vmem,
             vmem,
             vmem,
-            vmem,
+            pl.BlockSpec(memory_space=pltpu.HBM),
         ],
         out_specs=(vmem, vmem),
         scratch_shapes=[
             pltpu.VMEM((places, depth, cells), bf16),
+            pltpu.VMEM((picks, cells, cells), bf16),
             pltpu.VMEM((picks * depth, cells), f32),
             pltpu.VMEM((places * depth, cells), f32),
             pltpu.VMEM((BANDS, 2, 2, rows, depth, cells), bf16),
             pltpu.VMEM((BANDS, 2, 2, rows, depth, cells), bf16),
+            pltpu.VMEM((2, 2, rows, depth, cells), bf16),
             pltpu.VMEM((2, tile, depth, cells), bf16),
             pltpu.VMEM((2, tile, depth, cells), bf16),
             pltpu.VMEM((2, tile, depth, cells), bf16),
             pltpu.VMEM((2, tile, depth, cells), bf16),
             dma,
+            dma,
+            dma((2, 2)),
+            dma((2, 2)),
+            dma((2, 2)),
+            dma((2, 2)),
             dma((2, 2, 2)),
             dma((2, 2, 2)),
             dma((BANDS, 2, 2)),

time: 50.1 us -> 44.1 us (0.88)
  Pallas kernels: 42.8 us -> 36.5 us
    pallas_call x1, Pallas kernels: 42.8 us -> 36.5 us  [on_device(): pl.pallas_call(functools.partial(exchange, (lat_count, lon_count, rows, c...]
where the time goes in v2:
time: 44.1 us; the launch traced here: 43.5 us
  Pallas kernels  36.5 us (83%)
  local copies, waits for them, and re-layouts  5.62 us (13%)
  other arithmetic  0.77 us (2%)
  between operations  0.68 us (2%)
    pallas_call x1, Pallas kernels, on_device(): pl.pallas_call(functools.partial(exchange, (lat_count, lon_count, rows, c...  36.5 us
    unnamed x2, local copies, waits for them, and re-layouts  1.59 us
    transpose x1, local copies, waits for them, and re-layouts, on_device(): adjoint_forcing.transpose(2, 3, 0, 1, 4).reshape(tile, depth, cells)  1.02 us
    transpose x1, local copies, waits for them, and re-layouts, on_device(): own = perturbation.transpose(3, 2, 0, 1, 4).reshape(tile, depth, cells)  1.02 us
    reshape x1, local copies, waits for them, and re-layouts, on_device(): tangent.reshape(rows, cols, fields, levels, cells).transpose(2, 3, 0, 1, 4)  0.91 us
    reshape x1, local copies, waits for them, and re-layouts, on_device(): adjoint.reshape(cols, rows, fields, levels, cells).transpose(2, 3, 1, 0, 4)  0.91 us

profile of v2, /device:TPU:0, one launch (start us, length us, event | category | flops | bytes accessed | tf_op | source)
XLA Modules:
  0.0 43.5 jit_solution(1161273622480427869)
XLA Ops:
  0.6 0.7 %fusion.4 = s32[4,4,4]{2,1,0:T(4,128)S(1)} fusion(s32[4,4,4]{2,1,0:T(4,128)} %param.7, s32[4,4,4]{2,1,0:T(4,128)} %param.8, s32[]{:T(128)S(6)} %mul.15, s32[]{:T(128)S(6)} %mul.13), kind=kLoop, calls=%fused_computation.15 | loop fusion | flops 2432 | bytes 776 | tf_op jit(solution)/shard_map/add | solution.py:378
  1.4 0.1 reshape.24.where_ref
  1.5 0.1 eq.19
  1.6 1.0 %copy.7 = bf16[4,4,2,32,128]{4,3,2,1,0:T(8,128)(2,1)S(1)} copy(bf16[4,4,2,32,128]{4,0,1,3,2:T(4,128)(2,1)} %bitcast.18) | data formatting | bytes 524288 | tf_op jit(solution)/shard_map/transpose | solution.py:382
  2.6 1.0 %copy.8 = bf16[4,4,2,32,128]{4,3,2,1,0:T(8,128)(2,1)S(1)} copy(bf16[4,4,2,32,128]{4,1,0,3,2:T(4,128)(2,1)} %bitcast.19) | data formatting | bytes 524288 | tf_op jit(solution)/shard_map/transpose | solution.py:383
  3.6 0.0 copy-start
  3.7 1.6 %copy-done = bf16[4,4,4,128,128]{4,3,2,1,0:T(8,128)(2,1)S(1)} copy-done((bf16[4,4,4,128,128]{4,3,2,1,0:T(8,128)(2,1)S(1)}, bf16[4,4,4,128,128]{4,3,2,1,0:T(8,128)(2,1)}, u32[]{:S(2)}) %copy-start) | copy-done | bytes 2097176
  5.2 36.5 %exchange.1 = (bf16[16,64,128]{2,1,0:T(8,128)(2,1)S(1)}, bf16[16,64,128]{2,1,0:T(8,128)(2,1)S(1)}) custom-call(s32[64]{0:T(128)S(1)} %reshape.24.where_ref, bf16[16,64,128]{2,1,0:T(8,128)(2,1)S(1)} %bitcast.14, bf16[16,64,128]{2,1,0:T(8,128)(2,1)S(1)} %bitcast.15, bf16[160,128]{1,0:T(8,128)(2,1)S(1)} %fusion.onehot_ref, bf16[64,128,128]{2,1,0:T(8,128)(2,1)S(1)} %bitcast.13), custom_call_target="tpu_custom_call" | custom-call | tf_op jit(solution)/shard_map/exchange/pallas_call | solution.py:389
  41.7 0.9 %copy.14 = bf16[4,4,2,32,128]{4,1,0,3,2:T(4,128)(2,1)} copy(bf16[4,4,2,32,128]{4,3,2,1,0:T(8,128)(2,1)S(1)} %bitcast.17) | data formatting | bytes 524288 | tf_op jit(solution)/shard_map/reshape | solution.py:436
  42.6 0.9 %copy.13 = bf16[4,4,2,32,128]{4,0,1,3,2:T(4,128)(2,1)} copy(bf16[4,4,2,32,128]{4,3,2,1,0:T(8,128)(2,1)S(1)} %bitcast.16) | data formatting | bytes 524288 | tf_op jit(solution)/shard_map/reshape | solution.py:437
  (2 shorter events, 0.0 us)
Async XLA Ops:
  3.6 1.6 %copy-start = (bf16[4,4,4,128,128]{4,3,2,1,0:T(8,128)(2,1)S(1)}, bf16[4,4,4,128,128]{4,3,2,1,0:T(8,128)(2,1)}, u32[]{:S(2)}) copy-start(bf16[4,4,4,128,128]{4,3,2,1,0:T(8,128)(2,1)} %param.9) | copy-start | bytes 6291460

commit v3 on v2

--- a/solution.py
+++ b/solution.py
@@ -111,12 +111,12 @@
             device_id_type=MESH,
         )
 
-    def az_copy(d, near):
-        return pltpu.make_async_remote_copy(
-            src_ref=(near_out if near else far_out).at[d],
-            dst_ref=(near_in if near else far_in).at[d],
-            send_sem=az_send.at[d, near],
-            recv_sem=az_recv.at[d, near],
+    def az_copy(d, near, part):
+        return pltpu.make_async_remote_copy(
+            src_ref=(near_out if near else far_out).at[d, part],
+            dst_ref=(near_in if near else far_in).at[d, part],
+            send_sem=az_send.at[d, near, part],
+            recv_sem=az_recv.at[d, near, part],
             device_id={"lat": z + steps[d]},
             device_id_type=MESH,
         )
@@ -234,7 +234,7 @@
     for pole, step in poles:
         @pl.when(z == pole)
         def _():
-            for i in range(2):
+            for i in (1, 0):
                 for side in range(2):
                     ax_start(lend_copy(pole, step, i, side), (i + 1) * step, side, 0)
     for band in (2, -2):
@@ -249,27 +249,54 @@
                 def _():
                     z_copy(d, 1, part).start()
         x_all(x_copy, -steps[d], start)
+
+    borrows = {step: z == pole + step for pole, step in poles}
+    for step in steps:
+        if lending:
+            @pl.when(jnp.logical_not(borrows[step]))
+            def _():
+                x_all(ax_copy, step, ax_start)
+        else:
+            x_all(ax_copy, step, ax_start)
     x_all(x_copy, 0, wait_recv, (0,))
     for pole, step in poles:
         @pl.when(z == pole + step)
         def _():
             for side in range(2):
                 fwd_copy(pole, step, 0, side).start()
-            for i in range(2):
-                for side in range(2):
-                    lend_copy(pole, step, i, side).wait_recv()
-                    here = at(place(i * step, away(side, 0)), rows)
-                    value = lent[i, side].astype(jnp.float32)
-                    spread[here, :] += value.reshape(rows * depth, cells)
-    for band in (1, -1):
-        x_all(ax_copy, band, ax_start)
+
+    for d in range(2):
+        x_all(ax_copy, 2 * steps[d], ax_finish)
+
+        @pl.when(there(2 * steps[d]))
+        def _():
+            for part in range(cols):
+                here = at(place(2 * steps[d], HALO + part), rows)
+                value = spread[here, :].astype(jnp.bfloat16)
+                far_out[d, part] = value.reshape(rows, depth, cells)
+                az_copy(d, 0, part).start()
+
+    def borrow(pole, step, i):
+        for side in range(2):
+            lend_copy(pole, step, i, side).wait_recv()
+            here = at(place(i * step, away(side, 0)), rows)
+            value = lent[i, side].astype(jnp.float32)
+            spread[here, :] += value.reshape(rows * depth, cells)
+
+    for pole, step in poles:
+        @pl.when(z == pole + step)
+        def _():
+            borrow(pole, step, 1)
+            x_all(ax_copy, step, ax_start)
+            borrow(pole, step, 0)
+    x_all(ax_copy, 0, ax_start)
+
     for d in range(2):
         @pl.when(there(-2 * steps[d]))
         def _():
             for part in range(2):
                 z_copy(d, 1, part).wait_recv()
         x_all(x_copy, -2 * steps[d], start)
-    x_all(ax_copy, 0, ax_start)
     for band in (1, -1):
         x_all(x_copy, band, wait_recv, (0,))
     for pole, step in poles:
@@ -279,27 +306,22 @@
                 fwd_copy(pole, step, 1, side).start()
 
     for d in range(2):
-        x_all(ax_copy, 2 * steps[d], ax_finish)
-
-        @pl.when(there(2 * steps[d]))
-        def _():
-            value = spread[at(place(2 * steps[d], HALO), tile), :].astype(jnp.bfloat16)
-            far_out[d] = value.reshape(tile, depth, cells)
-            az_copy(d, 0).start()
-    for d in range(2):
         x_all(ax_copy, steps[d], ax_finish)
 
         @pl.when(there(steps[d]))
         def _():
-            here = at(place(steps[d], HALO), tile)
-
-            @pl.when(there(-steps[d]))
-            def _():
-                az_copy(d, 0).wait_recv()
-                spread[here, :] += far_in[d].astype(jnp.float32).reshape(tile * depth, cells)
-
-            near_out[d] = spread[here, :].astype(jnp.bfloat16).reshape(tile, depth, cells)
-            az_copy(d, 1).start()
+            for part in range(cols):
+                here = at(place(steps[d], HALO + part), rows)
+
+                @pl.when(there(-steps[d]))
+                def _():
+                    az_copy(d, 0, part).wait_recv()
+                    value = far_in[d, part].astype(jnp.float32)
+                    spread[here, :] += value.reshape(rows * depth, cells)
+
+                value = spread[here, :].astype(jnp.bfloat16)
+                near_out[d, part] = value.reshape(rows, depth, cells)
+                az_copy(d, 1, part).start()
 
     own_copy.wait()
     for band in range(-REACH, REACH + 1):
@@ -327,7 +349,8 @@
     for d in range(2):
         @pl.when(there(-steps[d]))
         def _():
-            az_copy(d, 1).wait_recv()
+            for part in range(cols):
+                az_copy(d, 1, part).wait_recv()
             spread[here, :] += near_in[d].astype(jnp.float32).reshape(tile * depth, cells)
     adjoint_ref[...] = spread[here, :].astype(jnp.bfloat16).reshape(tile, depth, cells)
 
@@ -349,7 +372,8 @@
         def _():
             for part in range(2):
                 z_copy(d, 0, part).wait_send()
-            az_copy(d, 1).wait_send()
+            for part in range(cols):
+                az_copy(d, 1, part).wait_send()
 
             @pl.when(there(-steps[d]))
             def _():
@@ -358,7 +382,8 @@
 
         @pl.when(there(2 * steps[d]))
         def _():
-            az_copy(d, 0).wait_send()
+            for part in range(cols):
+                az_copy(d, 0, part).wait_send()
 
 
 def on_device(perturbation, adjoint_forcing, source_rows, source_cols, cubic_weights):
@@ -381,7 +406,9 @@
     onehot = onehot.astype(jnp.bfloat16)
     own = perturbation.transpose(3, 2, 0, 1, 4).reshape(tile, depth, cells)
     forcing = adjoint_forcing.transpose(2, 3, 0, 1, 4).reshape(tile, depth, cells)
-    weights = cubic_weights.reshape(picks, cells, cells)
+    weights = pltpu.with_memory_space_constraint(
+        cubic_weights.reshape(picks, cells, cells), pltpu.HBM
+    )
 
     vmem = pl.BlockSpec(memory_space=pltpu.VMEM)
     dma = pltpu.SemaphoreType.DMA
@@ -409,10 +436,10 @@
             pltpu.VMEM((BANDS, 2, 2, rows, depth, cells), bf16),
             pltpu.VMEM((BANDS, 2, 2, rows, depth, cells), bf16),
             pltpu.VMEM((2, 2, rows, depth, cells), bf16),
-            pltpu.VMEM((2, tile, depth, cells), bf16),
-            pltpu.VMEM((2, tile, depth, cells), bf16),
-            pltpu.VMEM((2, tile, depth, cells), bf16),
-            pltpu.VMEM((2, tile, depth, cells), bf16),
+            pltpu.VMEM((2, cols, rows, depth, cells), bf16),
+            pltpu.VMEM((2, cols, rows, depth, cells), bf16),
+            pltpu.VMEM((2, cols, rows, depth, cells), bf16),
+            pltpu.VMEM((2, cols, rows, depth, cells), bf16),
             dma,
             dma,
             dma((2, 2)),
@@ -425,8 +452,8 @@
             dma((BANDS, 2, 2)),
             dma((BANDS, 2, 2)),
             dma((BANDS, 2, 2)),
-            dma((2, 2)),
-            dma((2, 2)),
+            dma((2, 2, cols)),
+            dma((2, 2, cols)),
         ],
         compiler_params=pltpu.CompilerParams(
             collective_id=0, has_side_effects=True, vmem_limit_bytes=48 * 1024 * 1024

time: 44.1 us -> 42.7 us (0.968)
  local copies, waits for them, and re-layouts: 5.62 us -> 4.03 us
    unnamed x2 -> x0, local copies, waits for them, and re-layouts: 1.59 us -> none
    pallas_call x1, Pallas kernels: 36.5 us -> 36.9 us  [on_device(): pl.pallas_call(functools.partial(exchange, (lat_count, lon_count, rows, c...]
where the time goes in v3:
time: 42.7 us; the launch traced here: 42.4 us
  Pallas kernels  36.9 us (86%)
  local copies, waits for them, and re-layouts  4.03 us (9%)
  other arithmetic  0.77 us (2%)
  between operations  0.67 us (2%)
    pallas_call x1, Pallas kernels, on_device(): pl.pallas_call(functools.partial(exchange, (lat_count, lon_count, rows, c...  36.9 us
    transpose x1, local copies, waits for them, and re-layouts, on_device(): own = perturbation.transpose(3, 2, 0, 1, 4).reshape(tile, depth, cells)  1.02 us
    transpose x1, local copies, waits for them, and re-layouts, on_device(): adjoint_forcing.transpose(2, 3, 0, 1, 4).reshape(tile, depth, cells)  1.02 us
    reshape x1, local copies, waits for them, and re-layouts, on_device(): tangent.reshape(rows, cols, fields, levels, cells).transpose(2, 3, 0, 1, 4)  0.91 us
    reshape x1, local copies, waits for them, and re-layouts, on_device(): adjoint.reshape(cols, rows, fields, levels, cells).transpose(2, 3, 1, 0, 4)  0.91 us

profile of v3, /device:TPU:0, one launch (start us, length us, event | category | flops | bytes accessed | tf_op | source)
XLA Modules:
  0.0 42.4 jit_solution(7850376929190481094)
XLA Ops:
  0.6 0.7 %fusion.4 = s32[4,4,4]{2,1,0:T(4,128)S(1)} fusion(s32[4,4,4]{2,1,0:T(4,128)} %param.7, s32[4,4,4]{2,1,0:T(4,128)} %param.8, s32[]{:T(128)S(6)} %mul.15, s32[]{:T(128)S(6)} %mul.13), kind=kLoop, calls=%fused_computation.15 | loop fusion | flops 2432 | bytes 776 | tf_op jit(solution)/shard_map/add | solution.py:403
  1.4 0.1 reshape.24.where_ref
  1.5 0.1 eq.19
  1.6 1.0 %copy.7 = bf16[4,4,2,32,128]{4,3,2,1,0:T(8,128)(2,1)S(1)} copy(bf16[4,4,2,32,128]{4,0,1,3,2:T(4,128)(2,1)} %bitcast.18) | data formatting | bytes 524288 | tf_op jit(solution)/shard_map/transpose | solution.py:407
  2.6 1.0 %copy.8 = bf16[4,4,2,32,128]{4,3,2,1,0:T(8,128)(2,1)S(1)} copy(bf16[4,4,2,32,128]{4,1,0,3,2:T(4,128)(2,1)} %bitcast.19) | data formatting | bytes 524288 | tf_op jit(solution)/shard_map/transpose | solution.py:408
  3.6 36.9 %exchange.1 = (bf16[16,64,128]{2,1,0:T(8,128)(2,1)S(1)}, bf16[16,64,128]{2,1,0:T(8,128)(2,1)S(1)}) custom-call(s32[64]{0:T(128)S(1)} %reshape.24.where_ref, bf16[16,64,128]{2,1,0:T(8,128)(2,1)S(1)} %bitcast.13, bf16[16,64,128]{2,1,0:T(8,128)(2,1)S(1)} %bitcast.14, bf16[160,128]{1,0:T(8,128)(2,1)S(1)} %fusion.onehot_ref, bf16[64,128,128]{2,1,0:T(8,128)(2,1)} %bitcast.17), custom_call_target="tpu_custom_call" | custom-call | tf_op jit(solution)/shard_map/exchange/pallas_call | solution.py:416
  40.6 0.9 %copy.14 = bf16[4,4,2,32,128]{4,1,0,3,2:T(4,128)(2,1)} copy(bf16[4,4,2,32,128]{4,3,2,1,0:T(8,128)(2,1)S(1)} %bitcast.16) | data formatting | bytes 524288 | tf_op jit(solution)/shard_map/reshape | solution.py:463
  41.5 0.9 %copy.13 = bf16[4,4,2,32,128]{4,0,1,3,2:T(4,128)(2,1)} copy(bf16[4,4,2,32,128]{4,3,2,1,0:T(8,128)(2,1)S(1)} %bitcast.15) | data formatting | bytes 524288 | tf_op jit(solution)/shard_map/reshape | solution.py:464
  (2 shorter events, 0.0 us)
